TPU v7x, 8 devices: a whole 2x2x1 slice. The times are simulated.
8 devices in a mesh: rep: 1 (over z), heads: 2 (over y), pool: 4 (over x, core).
Axes of the slice: x: 2, y: 2, z: 1, core: 2. Of those that a mesh axis runs over, the one named last changes fastest.
Arguments:
- kv_pool: bfloat16 [2, 512, 2, 32, 8, 128], P(None, ('rep', 'pool'), None, None, 'heads')
- page_idx: int32 [4, 4, 4], P('rep', 'pool')
- x_tokens: bfloat16 [4, 256, 5120], P(('rep', 'pool'))
- gain_attn: bfloat16 [2, 5120], replicated
- w_q: bfloat16 [2, 5120, 5120], P(None, None, 'heads')
- w_k: bfloat16 [2, 5120, 1024], P(None, None, 'heads')
- w_v: bfloat16 [2, 5120, 1024], P(None, None, 'heads')
- w_o: bfloat16 [2, 5120, 5120], P(None, 'heads')
- gain_mlp: bfloat16 [2, 5120], replicated
- w_gate: bfloat16 [2, 5120, 13824], P(None, None, 'heads')
- w_up: bfloat16 [2, 5120, 13824], P(None, None, 'heads')
- w_down: bfloat16 [2, 13824, 5120], P(None, 'heads')
Outputs:
- output: bfloat16 [4, 256, 5120], P(('rep', 'pool'))
All inputs are finite; a program needn't handle non-finite values.
Results may differ from a plain program's by a relative error of at most 0.02.
Values are sent between devices in bfloat16 or wider.
A program may use at most 2.25 GiB of HBM per device.

v0:
```python
import jax
import jax.numpy as jnp
from jax import lax
from jax.sharding import PartitionSpec as P


def rms_norm(hidden, gain_vec):
    hid_f32 = hidden.astype(jnp.float32)
    inv_rms = lax.rsqrt(jnp.mean(hid_f32 * hid_f32, axis=-1, keepdims=True) + 1e-5)
    return (hid_f32 * inv_rms * gain_vec.astype(jnp.float32)).astype(jnp.bfloat16)


def rope_tables(prefix, tokens, head_dim):
    positions = (prefix + jnp.arange(tokens)).astype(jnp.float32)
    inv_freq = 10000.0 ** (-2.0 * jnp.arange(head_dim // 2).astype(jnp.float32) / head_dim)
    angles = positions[:, None] * inv_freq[None, :]
    return jnp.cos(angles)[:, None, :], jnp.sin(angles)[:, None, :]


def apply_rope(projected, cos_tab, sin_tab):
    half_dim = projected.shape[-1] // 2
    first_half = projected[..., :half_dim]
    second_half = projected[..., half_dim:]
    return jnp.concatenate([first_half * cos_tab - second_half * sin_tab, second_half * cos_tab + first_half * sin_tab], axis=-1)


def attend(queries, keys_pre, vals_pre, k_new, v_new, causal):
    score_scale = queries.shape[-1] ** -0.5
    s_pre = jnp.einsum('tgrd,ngd->grtn', queries, keys_pre, preferred_element_type=jnp.float32) * score_scale
    s_new = jnp.einsum('tgrd,ngd->grtn', queries, k_new, preferred_element_type=jnp.float32) * score_scale
    s_new = jnp.where(causal, s_new, -jnp.inf)
    row_max = jnp.maximum(jnp.max(s_pre, axis=-1, keepdims=True), jnp.max(s_new, axis=-1, keepdims=True))
    e_pre = jnp.exp(s_pre - row_max)
    e_new = jnp.exp(s_new - row_max)
    inv_den = 1.0 / (jnp.sum(e_pre, axis=-1, keepdims=True) + jnp.sum(e_new, axis=-1, keepdims=True))
    p_pre = (e_pre * inv_den).astype(jnp.bfloat16)
    p_new = (e_new * inv_den).astype(jnp.bfloat16)
    attn_sum = jnp.einsum('grtn,ngd->tgrd', p_pre, vals_pre, preferred_element_type=jnp.float32)
    attn_sum = attn_sum + jnp.einsum('grtn,ngd->tgrd', p_new, v_new, preferred_element_type=jnp.float32)
    return attn_sum.astype(jnp.bfloat16)


def solution(mesh):
    owners = mesh.shape['pool']

    def local_fn(kv_pool, page_idx, x_tokens, gain_attn, w_q, w_k, w_v, w_o, gain_mlp, w_gate, w_up, w_down):
        layers, _, _, page_len, kv_loc, head_dim = kv_pool.shape
        tokens = x_tokens.shape[1]
        req_pages = page_idx.shape[2]
        q_loc = w_q.shape[2] // head_dim
        group_q = q_loc // kv_loc
        prefix = owners * req_pages * page_len
        wanted = page_idx.reshape(owners * req_pages)
        cos_tab, sin_tab = rope_tables(prefix, tokens, head_dim)
        causal = jnp.arange(tokens)[:, None] >= jnp.arange(tokens)[None, :]
        hidden = x_tokens[0]
        for layer_id in range(layers):
            picked = jnp.take(kv_pool[layer_id], wanted, axis=0)
            received = lax.all_to_all(picked, 'pool', 0, 0, tiled=True)
            keys_pre = received[:, 0].reshape(prefix, kv_loc, head_dim)
            vals_pre = received[:, 1].reshape(prefix, kv_loc, head_dim)
            h_att = rms_norm(hidden, gain_attn[layer_id])
            q_proj = jnp.dot(h_att, w_q[layer_id], preferred_element_type=jnp.float32).reshape(tokens, q_loc, head_dim)
            k_proj = jnp.dot(h_att, w_k[layer_id], preferred_element_type=jnp.float32).reshape(tokens, kv_loc, head_dim)
            queries = apply_rope(q_proj, cos_tab, sin_tab).astype(jnp.bfloat16).reshape(tokens, kv_loc, group_q, head_dim)
            k_new = apply_rope(k_proj, cos_tab, sin_tab).astype(jnp.bfloat16)
            v_new = jnp.dot(h_att, w_v[layer_id], preferred_element_type=jnp.float32).astype(jnp.bfloat16).reshape(tokens, kv_loc, head_dim)
            attn_cat = attend(queries, keys_pre, vals_pre, k_new, v_new, causal).reshape(tokens, q_loc * head_dim)
            attn_out = lax.psum(jnp.dot(attn_cat, w_o[layer_id], preferred_element_type=jnp.float32), 'heads')
            x_mid = (hidden.astype(jnp.float32) + attn_out).astype(jnp.bfloat16)
            h_mlp = rms_norm(x_mid, gain_mlp[layer_id])
            gate_proj = jnp.dot(h_mlp, w_gate[layer_id], preferred_element_type=jnp.float32)
            up_proj = jnp.dot(h_mlp, w_up[layer_id], preferred_element_type=jnp.float32)
            act_out = (jax.nn.silu(gate_proj) * up_proj).astype(jnp.bfloat16)
            mlp_out = lax.psum(jnp.dot(act_out, w_down[layer_id], preferred_element_type=jnp.float32), 'heads')
            hidden = (x_mid.astype(jnp.float32) + mlp_out).astype(jnp.bfloat16)
        return hidden[None]

    pool_spec = P(None, ('rep', 'pool'), None, None, 'heads', None)
    index_spec = P('rep', 'pool', None)
    x_spec = P(('rep', 'pool'), None, None)
    gain_spec = P(None, None)
    col_spec = P(None, None, 'heads')
    row_spec = P(None, 'heads', None)
    return jax.shard_map(local_fn, mesh=mesh, in_specs=(pool_spec, index_spec, x_spec, gain_spec, col_spec, col_spec, col_spec, row_spec, gain_spec, col_spec, col_spec, row_spec), out_specs=x_spec, check_vma=False)
```

profile of v0, /device:TPU:0, one launch (start us, length us, event | category | flops | bytes accessed | tf_op | source)
XLA Modules:
  0.0 960.0 jit_solution(11047355030316874257)
XLA Ops:
  8.5 11.1 %fusion.153 = (bf16[1,128,2,32,4,128]{5,4,3,2,1,0:T(4,128)(2,1)S(1)}, bf16[1,128,2,32,4,128]{5,4,3,2,1,0:T(4,128)(2,1)S(1)}) fusion(bf16[2,128,2,32,4,128]{5,4,3,2,1,0:T(4,128)(2,1)} %param.14), kind=kLoop, calls=%fused_computation.185 | loop fusion | bytes 33554432 | tf_op jit(solution)/shard_map/slice | solution.py:58
  19.6 7.7 copy_bitcast_fusion
  27.3 5.3 gather_fusion
  32.6 5.0 gather_fusion.1
  40.7 4.6 all-to-all-start
  46.6 34.7 %slice_bitcast_fusion = (bf16[2560,5120]{0,1:T(8,128)(2,1)}, bf16[2560,5120]{0,1:T(8,128)(2,1)}) fusion(bf16[2,5120,2560]{2,1,0:T(8,128)(2,1)} %param.18), kind=kLoop, calls=%fused_computation.25 | loop fusion | bytes 104857600 | tf_op jit(solution)/shard_map/dot_general | solution.py:63
  81.3 35.2 %copy.54 = bf16[2560,5120]{1,0:T(8,128)(2,1)} copy(bf16[2560,5120]{0,1:T(8,128)(2,1)} %get-tuple-element.13) | data formatting | bytes 52428800 | tf_op jit(solution)/shard_map/dot_general | solution.py:63
  116.5 8.6 slice_bitcast_fusion.2
  125.1 7.9 copy.57
  132.9 12.6 %fusion.97 = f32[256,20,128]{0,2,1:T(8,128)S(1)} fusion(bf16[20,128,5120]{2,1,0:T(8,128)(2,1)} %bitcast.227, bf16[1,256,5120]{2,1,0:T(8,128)(2,1)S(1)} %copy-done.2, f32[5120]{0:T(1024)S(1)} %bitcast.249, f32[256]{0:T(256)S(1)} %add_rsqrt_fusion.3), kind=kOutput, calls=%fused_computation.116 | convolution fusion | flops 6716129280 | bytes 31478784 | tf_op jit(solution)/shard_map/dot_general | solution.py:63
  148.1 4.7 fusion.113
  172.3 13.6 %fusion.20 = f32[256,5120]{1,0:T(8,128)} fusion(bf16[256,2560]{0,1:T(8,128)(2,1)S(1)} %bitcast.240, bf16[2,2560,5120]{2,1,0:T(8,128)(2,1)} %param.21), kind=kOutput, calls=%fused_computation.22 | convolution fusion | flops 6710886400 | bytes 32768000 | tf_op jit(solution)/shard_map/dot_general | solution.py:69
  187.2 126.5 %all-reduce.5.cloned.1.call-done = f32[256,5120]{1,0:T(8,128)} async-done(((f32[256,5120]{1,0:T(8,128)}), f32[256,5120]{1,0:T(8,128)}) %all-reduce.5.cloned.1.call-update) | async-done | bytes 5242896 | tf_op jit(solution)/shard_map/psum | solution.py:69
  313.8 5.0 fusion.56
  318.8 35.8 %fusion.10 = f32[256,6912]{1,0:T(8,128)} fusion(bf16[2,5120,6912]{2,1,0:T(8,128)(2,1)} %param.23, bf16[256,5120]{1,0:T(8,128)(2,1)} %get-tuple-element.11, f32[5120]{0:T(1024)S(1)} %bitcast.252, f32[256]{0:T(256)S(1)} %add_rsqrt_fusion.2), kind=kOutput, calls=%fused_computation.12 | convolution fusion | flops 18124636160 | bytes 80499712 | tf_op jit(solution)/shard_map/dot_general | solution.py:72
  354.6 30.9 %fusion.35.clone.5 = bf16[256,6912]{1,0:T(8,128)(2,1)} fusion(bf16[2,5120,6912]{2,1,0:T(8,128)(2,1)} %param.24, f32[256,6912]{1,0:T(8,128)} %fusion.10, bf16[256,5120]{1,0:T(8,128)(2,1)S(1)} %copy-done.5, f32[5120]{0:T(1024)S(1)} %bitcast.253, f32[256]{0:T(256)S(1)} %add_rsqrt_fusion.2), kind=kOutput, calls=%fused_computation.39.clone.clone.clone.2 | convolution fusion | flops 18135252992 | bytes 84038656 | tf_op jit(solution)/shard_map/dot_general | solution.py:73
  385.6 29.9 %fusion.6 = f32[256,5120]{1,0:T(8,128)} fusion(bf16[2,6912,5120]{2,1,0:T(8,128)(2,1)} %param.25, bf16[256,6912]{1,0:T(8,128)(2,1)} %fusion.35.clone.5), kind=kOutput, calls=%fused_computation.8 | convolution fusion | flops 18119393280 | bytes 79560704 | tf_op jit(solution)/shard_map/dot_general | solution.py:75
  419.8 35.3 %copy.66 = bf16[2560,5120]{1,0:T(8,128)(2,1)} copy(bf16[2560,5120]{0,1:T(8,128)(2,1)} %get-tuple-element.12) | data formatting | bytes 52428800 | tf_op jit(solution)/shard_map/dot_general | solution.py:63
  455.2 8.0 copy.69
  466.2 74.2 %all-reduce.7.cloned.1.call-done = f32[256,5120]{1,0:T(8,128)} async-done(((f32[256,5120]{1,0:T(8,128)}), f32[256,5120]{1,0:T(8,128)}) %all-reduce.7.cloned.1.call-update) | async-done | bytes 5242896 | tf_op jit(solution)/shard_map/psum | solution.py:75
  543.9 5.7 fusion.110
  549.7 12.7 %fusion.93 = f32[256,20,128]{0,2,1:T(8,128)S(1)} fusion(bf16[20,128,5120]{2,1,0:T(8,128)(2,1)} %bitcast.226, bf16[256,5120]{1,0:T(8,128)(2,1)S(1)} %get-tuple-element.9, f32[5120]{0:T(1024)S(1)} %bitcast.245, f32[256]{0:T(256)S(1)} %add_rsqrt_fusion.1), kind=kOutput, calls=%fused_computation.112 | convolution fusion | flops 6716129280 | bytes 31478784 | tf_op jit(solution)/shard_map/dot_general | solution.py:63
  564.4 5.0 fusion.91
  583.1 6.5 add_convert_fusion
  589.6 13.6 %fusion.18 = f32[256,5120]{1,0:T(8,128)} fusion(bf16[256,2560]{0,1:T(8,128)(2,1)S(1)} %bitcast.241, bf16[2,2560,5120]{2,1,0:T(8,128)(2,1)} %param.21), kind=kOutput, calls=%fused_computation.20 | convolution fusion | flops 6710886400 | bytes 32768000 | tf_op jit(solution)/shard_map/dot_general | solution.py:69
  603.2 124.8 %all-reduce.9.cloned.1.call-done = f32[256,5120]{1,0:T(8,128)} async-done(((f32[256,5120]{1,0:T(8,128)}), f32[256,5120]{1,0:T(8,128)}) %all-reduce.9.cloned.1.call-update) | async-done | bytes 5242896 | tf_op jit(solution)/shard_map/psum | solution.py:69
  728.1 4.3 fusion.64
  732.5 30.2 %fusion.4 = f32[256,6912]{1,0:T(8,128)} fusion(bf16[2,5120,6912]{2,1,0:T(8,128)(2,1)} %param.23, bf16[256,5120]{1,0:T(8,128)(2,1)S(1)} %get-tuple-element.7, f32[5120]{0:T(1024)S(1)} %bitcast.247, f32[256]{0:T(256)S(1)} %add_rsqrt_fusion), kind=kOutput, calls=%fused_computation.6 | convolution fusion | flops 18124636160 | bytes 80499712 | tf_op jit(solution)/shard_map/dot_general | solution.py:72
  762.6 30.9 %fusion.32.clone.5 = bf16[256,6912]{1,0:T(8,128)(2,1)} fusion(bf16[2,5120,6912]{2,1,0:T(8,128)(2,1)} %param.24, f32[256,6912]{1,0:T(8,128)} %fusion.4, bf16[256,5120]{1,0:T(8,128)(2,1)S(1)} %get-tuple-element.7, f32[5120]{0:T(1024)S(1)} %bitcast.248, f32[256]{0:T(256)S(1)} %add_rsqrt_fusion), kind=kOutput, calls=%fused_computation.38.clone.clone.clone.2 | convolution fusion | flops 18135252992 | bytes 84038656 | tf_op jit(solution)/shard_map/dot_general | solution.py:73
  793.5 30.0 %fusion = f32[256,5120]{1,0:T(8,128)} fusion(bf16[2,6912,5120]{2,1,0:T(8,128)(2,1)} %param.25, bf16[256,6912]{1,0:T(8,128)(2,1)} %fusion.32.clone.5), kind=kOutput, calls=%fused_computation.2 | convolution fusion | flops 18119393280 | bytes 79560704 | tf_op jit(solution)/shard_map/dot_general | solution.py:75
  823.5 124.9 %all-reduce.11.cloned.1.call-done = f32[256,5120]{1,0:T(8,128)} async-done(((f32[256,5120]{1,0:T(8,128)}), f32[256,5120]{1,0:T(8,128)}) %all-reduce.11.cloned.1.call-update) | async-done | bytes 5242896 | tf_op jit(solution)/shard_map/psum | solution.py:75
  948.4 4.7 fusion.90
  (107 shorter events, 56.0 us)
Async XLA Ops:
  27.3 18.1 %copy-start.16 = (bf16[2,5120]{1,0:T(2,128)(2,1)S(1)}, bf16[2,5120]{1,0:T(2,128)(2,1)}, u32[]{:S(2)}) copy-start(bf16[2,5120]{1,0:T(2,128)(2,1)} %param.17) | copy-start | bytes 61444
  27.3 18.7 %copy-start.2 = (bf16[1,256,5120]{2,1,0:T(8,128)(2,1)S(1)}, bf16[1,256,5120]{2,1,0:T(8,128)(2,1)}, u32[]{:S(2)}) copy-start(bf16[1,256,5120]{2,1,0:T(8,128)(2,1)} %param.16) | copy-start | bytes 7864324
  40.7 120.6 %all-to-all-start = ((bf16[16,2,32,4,128]{4,2,3,1,0:T(8,128)(2,1)}), bf16[16,2,32,4,128]{4,2,3,1,0:T(8,128)(2,1)}, u32[]{:S(2)}, u32[]{:S(2)}) async-start(bf16[16,2,32,4,128]{4,2,3,1,0:T(8,128)(2,1)} %get-tuple-element.37), calls=%async_computation | async-start | bytes 2097152 | tf_op jit(solution)/shard_map/all_to_all | solution.py:59
  45.3 268.4 %all-reduce.5.cloned.1.call-start = ((), (), s32[]{:S(2)}) async-start(), calls=%async_computation.2 | async-start | bytes 10485760 | tf_op jit(solution)/shard_map/psum | solution.py:69
  132.9 12.6 %copy-start.6 = (bf16[512,5120]{1,0:T(8,128)(2,1)S(1)}, bf16[512,5120]{1,0:T(8,128)(2,1)}, u32[]{:S(2)}) copy-start(bf16[512,5120]{1,0:T(8,128)(2,1)} %copy.57) | copy-start | bytes 15728644
  153.1 8.2 copy-start.11
  153.1 8.2 copy-start.13
  156.2 11.8 %copy-start.9 = (pred[256,256]{0,1:T(8,128)(4,1)}, pred[256,256]{0,1:T(8,128)(4,1)S(1)}, u32[]{:S(2)}) copy-start(pred[256,256]{0,1:T(8,128)(4,1)S(1)} %iota_compare_fusion) | copy-start | bytes 196612
  162.6 2.3 slice-start
  162.7 2.4 slice-start.1
  185.9 0.7 copy-start.17
  185.9 127.9 %copy-start.3 = (bf16[1,256,5120]{2,1,0:T(8,128)(2,1)S(1)}, bf16[1,256,5120]{2,1,0:T(8,128)(2,1)}, u32[]{:S(2)}) copy-start(bf16[1,256,5120]{2,1,0:T(8,128)(2,1)} %param.16) | copy-start | bytes 7864324
  185.9 354.5 %all-reduce.7.cloned.1.call-start = ((), (), s32[]{:S(2)}) async-start(), calls=%async_computation.3 | async-start | bytes 10485760 | tf_op jit(solution)/shard_map/psum | solution.py:75
  318.8 35.8 %copy-start.5 = (bf16[256,5120]{1,0:T(8,128)(2,1)S(1)}, bf16[256,5120]{1,0:T(8,128)(2,1)}, u32[]{:S(2)}) copy-start(bf16[256,5120]{1,0:T(8,128)(2,1)} %get-tuple-element.11) | copy-start | bytes 7864324
  415.5 47.7 %all-to-all-start.1 = ((bf16[16,2,32,4,128]{4,2,3,1,0:T(8,128)(2,1)}), bf16[16,2,32,4,128]{4,2,3,1,0:T(8,128)(2,1)}, u32[]{:S(2)}, u32[]{:S(2)}) async-start(bf16[16,2,32,4,128]{4,2,3,1,0:T(8,128)(2,1)} %get-tuple-element.36), calls=%async_computation.1 | async-start | bytes 2097152 | tf_op jit(solution)/shard_map/all_to_all | solution.py:59
  419.8 308.3 %all-reduce.9.cloned.1.call-start = ((), (), s32[]{:S(2)}) async-start(), calls=%async_computation.4 | async-start | bytes 10485760 | tf_op jit(solution)/shard_map/psum | solution.py:69
  466.2 77.8 %copy-start.18 = (f32[1,5120]{1,0:T(1,128)S(1)}, f32[1,5120]{1,0:T(1,128)}, u32[]{:S(2)}) copy-start(f32[1,5120]{1,0:T(1,128)} %get-tuple-element.32) | copy-start | bytes 61444
  543.9 5.8 copy-start.4
  549.7 12.7 %copy-start.12 = (f32[256,64]{0,1:T(8,128)S(1)}, f32[256,64]{0,1:T(8,128)}, u32[]{:S(2)}) copy-start(f32[256,64]{0,1:T(8,128)} %copy-done.11) | copy-start | bytes 196612
  549.7 12.7 %copy-start.14 = (f32[256,64]{0,1:T(8,128)S(1)}, f32[256,64]{0,1:T(8,128)}, u32[]{:S(2)}) copy-start(f32[256,64]{0,1:T(8,128)} %copy-done.13) | copy-start | bytes 196612
  564.4 5.1 copy-start.8
  569.4 2.2 copy-start.10
  571.6 5.5 copy-start
  573.2 2.8 copy-start.1
  577.1 1.8 copy-start.15
  578.9 4.2 copy-start.7
  603.2 129.3 %copy-start.19 = (f32[1,5120]{1,0:T(1,128)S(1)}, f32[1,5120]{1,0:T(1,128)}, u32[]{:S(2)}) copy-start(f32[1,5120]{1,0:T(1,128)} %get-tuple-element.30) | copy-start | bytes 61444
  603.2 345.2 %all-reduce.11.cloned.1.call-start = ((), (), s32[]{:S(2)}) async-start(), calls=%async_computation.5 | async-start | bytes 10485760 | tf_op jit(solution)/shard_map/psum | solution.py:75
Sparse Core Ops, SparseCore 0:
  186.0 127.6 all-reduce.4
  415.6 124.7 all-reduce.6
  603.3 124.7 all-reduce.8
  823.7 124.7 all-reduce.10
where the time goes:
time: 966 us; the launch traced here: 960 us
  waiting for transfers between devices  451 us (47%)
  matrix products  283 us (29%)
  local copies, waits for them, and re-layouts  172 us (18%)
  other arithmetic  32 us (3%)
  between operations  14.1 us (1%)
    psum x2, waiting for transfers between devices, local_fn(): lax.psum(jnp.dot(attn_cat, w_o[layer_id], preferred_element_type=jnp.floa...  251 us
    psum x2, waiting for transfers between devices, local_fn(): lax.psum(jnp.dot(act_out, w_down[layer_id], preferred_element_type=jnp.fl...  199 us
    dot_general x3, local copies, waits for them, and re-layouts, local_fn(): jnp.dot(h_att, w_q[layer_id], preferred_element_type=jnp.float32)  105 us
    dot_general x2, matrix products, local_fn(): jnp.dot(h_mlp, w_gate[layer_id], preferred_element_type=jnp.float32)  66 us
    dot_general x2, matrix products, local_fn(): up_proj = jnp.dot(h_mlp, w_up[layer_id], preferred_element_type=jnp.float32)  61.8 us
    dot_general x2, matrix products, local_fn(): jnp.dot(act_out, w_down[layer_id], preferred_element_type=jnp.float32)  59.9 us
    dot_general x2, matrix products, local_fn(): jnp.dot(attn_cat, w_o[layer_id], preferred_element_type=jnp.float32)  27.1 us
    dot_general x2, matrix products, local_fn(): jnp.dot(h_att, w_q[layer_id], preferred_element_type=jnp.float32)  25.3 us
  transfers between devices with their start and end apart: 6, of which 4 were waited for; matrix products, arithmetic and copies ran while one was open for 17% of the time, Pallas kernels for 0%

commit v1 on v0

v1 whole, which is shorter than its diff:
```python
import functools

import jax
import jax.numpy as jnp
from jax import lax
from jax.experimental import pallas as pl
from jax.experimental.pallas import tpu as pltpu
from jax.sharding import PartitionSpec as P

MESH = pl.DeviceIdType.MESH
F32 = jnp.float32
BF16 = jnp.bfloat16
TILE = 256
SLOTS = 9
AHEAD = SLOTS - 1


def rope_tables(prefix, tokens, head_dim):
    positions = (prefix + jnp.arange(tokens)).astype(F32)
    inv_freq = 10000.0 ** (-2.0 * jnp.arange(head_dim // 2).astype(F32) / head_dim)
    angles = positions[:, None] * inv_freq[None, :]
    cos_tab, sin_tab = jnp.cos(angles), jnp.sin(angles)
    return jnp.concatenate([cos_tab, cos_tab], axis=-1), jnp.concatenate([-sin_tab, sin_tab], axis=-1)


def layers_kernel(
    dims,
    kv_hbm, x_hbm, cos_ref, sin_ref, ga_ref, gm_ref,
    wq_hbm, wk_hbm, wv_hbm, wo_hbm, wg_hbm, wu_hbm, wd_hbm,
    out_hbm,
    ring, xbuf, hbuf, qbuf, kbuf, vbuf, abuf, ubuf, pbuf, rbuf, kvbuf,
    ring_sem, load_sem, rs_send, rs_recv, ag_send, ag_recv,
):
    layers, tokens, kv_loc, group_q, head_dim, width, ffn, prefix = dims
    q_loc = kv_loc * group_q
    rows = tokens // 2
    half = rows // 2
    per_tile = TILE // head_dim
    scale = head_dim ** -0.5

    me = lax.axis_index('heads')
    other = 1 - me

    n_q, n_kv = q_loc * head_dim // TILE, kv_loc * head_dim // TILE
    n_d, n_f = width // TILE, ffn // TILE
    attn_seq = [('q', n_q), ('k', n_kv), ('v', n_kv), ('o', n_d)]
    mlp_seq = [('gu', 2 * n_f), ('d', n_d)]
    phases = attn_seq + attn_seq + mlp_seq + mlp_seq
    bases = [sum(n for _, n in phases[:p]) for p in range(len(phases))]
    per_layer = sum(n for _, n in phases)
    q_rows = q_loc * head_dim

    def copies(kind, layer, idx, slot):
        def tile(w_hbm, depth, col):
            start = col * TILE if isinstance(col, int) else pl.multiple_of(col * TILE, TILE)
            return pltpu.make_async_copy(w_hbm.at[layer, :, pl.ds(start, TILE)], ring.at[slot, pl.ds(0, depth), :], ring_sem.at[slot])
        if kind == 'q':
            return tile(wq_hbm, width, idx)
        if kind == 'k':
            return tile(wk_hbm, width, idx)
        if kind == 'v':
            return tile(wv_hbm, width, idx)
        if kind == 'o':
            return tile(wo_hbm, q_rows, idx)
        if kind == 'g':
            return tile(wg_hbm, width, idx)
        if kind == 'u':
            return tile(wu_hbm, width, idx)
        return tile(wd_hbm, ffn, idx)

    def start_tile(phase, layer, idx, slot):
        kind = phases[phase][0]
        if kind != 'gu':
            copies(kind, layer, idx, slot).start()
        elif isinstance(idx, int):
            copies('gu'[idx % 2], layer, idx // 2, slot).start()
        else:
            @pl.when(lax.rem(idx, 2) == 0)
            def _():
                copies('g', layer, idx // 2, slot).start()

            @pl.when(lax.rem(idx, 2) == 1)
            def _():
                copies('u', layer, idx // 2, slot).start()

    def prefetch(phase, layer, idx):
        slot = lax.rem(layer * per_layer + bases[phase] + idx + AHEAD, SLOTS)
        lo = -AHEAD
        p, wrapped = phase, False
        count = phases[phase][1]
        while lo < count:
            hi = lo + phases[p][1]
            if hi > 0:
                local = idx - lo
                cond = (idx >= lo) & (idx < hi)
                target = layer + 1 if wrapped else layer
                if wrapped:
                    cond = cond & (target < layers)

                @pl.when(cond)
                def _(p=p, target=target, local=local):
                    start_tile(p, target, local, slot)
            lo = hi
            p += 1
            if p == len(phases):
                p, wrapped = 0, True

    def take(phase, layer, idx, kind, col):
        prefetch(phase, layer, idx)
        slot = lax.rem(layer * per_layer + bases[phase] + idx, SLOTS)
        copies(kind, layer, col, slot).wait()
        return slot

    def norm(chunk, gain_ref, layer):
        step = 16

        def body(i, carry):
            at = pl.multiple_of(chunk * rows + i * step, step)
            to = pl.multiple_of(i * step, step)
            hid = xbuf[pl.ds(at, step), :].astype(F32)
            inv = lax.rsqrt(jnp.mean(hid * hid, axis=-1, keepdims=True) + 1e-5)
            hbuf[pl.ds(to, step), :] = (hid * inv * gain_ref[layer]).astype(BF16)
            return carry

        lax.fori_loop(0, rows // step, body, 0)

    def roped(block, chunk):
        cos = cos_ref[chunk * rows:(chunk + 1) * rows, :]
        sin = sin_ref[chunk * rows:(chunk + 1) * rows, :]
        return (block * cos + pltpu.roll(block, head_dim // 2, 1) * sin).astype(BF16)

    def project(phase, chunk, layer):
        def q_body(i, carry):
            slot = take(phase, layer, i, 'q', i)
            res = jnp.dot(hbuf[...], ring[slot, :width, :], preferred_element_type=F32)
            for s in range(per_tile):
                qbuf[i * per_tile + s] = roped(res[:, s * head_dim:(s + 1) * head_dim], chunk)
            return carry

        def k_body(i, carry):
            slot = take(phase + 1, layer, i, 'k', i)
            res = jnp.dot(hbuf[...], ring[slot, :width, :], preferred_element_type=F32)
            for s in range(per_tile):
                kbuf[i * per_tile + s, chunk * rows:(chunk + 1) * rows, :] = roped(res[:, s * head_dim:(s + 1) * head_dim], chunk)
            return carry

        def v_body(i, carry):
            slot = take(phase + 2, layer, i, 'v', i)
            res = jnp.dot(hbuf[...], ring[slot, :width, :], preferred_element_type=F32)
            for s in range(per_tile):
                vbuf[i * per_tile + s, chunk * rows:(chunk + 1) * rows, :] = res[:, s * head_dim:(s + 1) * head_dim].astype(BF16)
            return carry

        lax.fori_loop(0, n_q, q_body, 0)
        lax.fori_loop(0, n_kv, k_body, 0)
        lax.fori_loop(0, n_kv, v_body, 0)

    def attend(chunk, layer):
        n_new = (chunk + 1) * rows
        nt = (((1,), (1,)), ((), ()))

        def body(g, carry):
            for r in range(group_q):
                q = qbuf[g * group_q + r]
                s_pre = lax.dot_general(q, kvbuf[layer, 0, g], nt, preferred_element_type=F32) * scale
                s_new = lax.dot_general(q, kbuf[g, :n_new, :], nt, preferred_element_type=F32) * scale
                tok = chunk * rows + lax.broadcasted_iota(jnp.int32, (rows, n_new), 0)
                key = lax.broadcasted_iota(jnp.int32, (rows, n_new), 1)
                s_new = jnp.where(key <= tok, s_new, -jnp.inf)
                top = jnp.maximum(jnp.max(s_pre, axis=-1, keepdims=True), jnp.max(s_new, axis=-1, keepdims=True))
                e_pre = jnp.exp(s_pre - top)
                e_new = jnp.exp(s_new - top)
                inv = 1.0 / (jnp.sum(e_pre, axis=-1, keepdims=True) + jnp.sum(e_new, axis=-1, keepdims=True))
                att = jnp.dot((e_pre * inv).astype(BF16), kvbuf[layer, 1, g], preferred_element_type=F32)
                att = att + jnp.dot((e_new * inv).astype(BF16), vbuf[g, :n_new, :], preferred_element_type=F32)
                col = pl.multiple_of((g * group_q + r) * head_dim, head_dim)
                abuf[:, pl.ds(col, head_dim)] = att.astype(BF16)
            return carry

        lax.fori_loop(0, kv_loc, body, 0)

    def send_block(chunk, col, cols):
        at = pl.multiple_of(other * half, half)
        return pltpu.make_async_remote_copy(
            src_ref=pbuf.at[chunk, pl.ds(at, half), pl.ds(col, cols)],
            dst_ref=rbuf.at[chunk, :, pl.ds(col, cols)],
            send_sem=rs_send.at[chunk],
            recv_sem=rs_recv.at[chunk],
            device_id={'heads': other},
            device_id_type=MESH,
        )

    def reduce_out(phase, chunk, layer, kind, src, depth):
        def body(i, carry):
            slot = take(phase, layer, i, kind, i)
            res = jnp.dot(src[...], ring[slot, :depth, :], preferred_element_type=F32)
            pbuf[chunk, :, pl.ds(pl.multiple_of(i * TILE, TILE), TILE)] = res

            @pl.when(i > 0)
            def _():
                send_block(chunk, pl.multiple_of((i - 1) * TILE, TILE), TILE).start()
            return carry

        lax.fori_loop(0, n_d, body, 0)
        send_block(chunk, width - TILE, TILE).start()

    def share(chunk):
        at = pl.multiple_of(chunk * rows + me * half, half)
        return pltpu.make_async_remote_copy(
            src_ref=xbuf.at[pl.ds(at, half), :],
            dst_ref=xbuf.at[pl.ds(at, half), :],
            send_sem=ag_send.at[chunk],
            recv_sem=ag_recv.at[chunk],
            device_id={'heads': other},
            device_id_type=MESH,
        )

    def reduce_and_share(chunk):
        whole = send_block(chunk, 0, width)
        whole.wait_recv()
        step = 16

        def body(i, carry):
            at = pl.multiple_of(chunk * rows + me * half + i * step, step)
            mine = pl.multiple_of(me * half + i * step, step)
            got = pl.multiple_of(i * step, step)
            total = pbuf[chunk, pl.ds(mine, step), :] + rbuf[chunk, pl.ds(got, step), :]
            xbuf[pl.ds(at, step), :] = (xbuf[pl.ds(at, step), :].astype(F32) + total).astype(BF16)
            return carry

        lax.fori_loop(0, half // step, body, 0)
        whole.wait_send()
        share(chunk).start()

    def shared(chunk):
        share(chunk).wait()

    def gate_up(phase, layer, first, last):
        def body(i, carry):
            slot = take(phase, layer, 2 * i, 'g', i)
            gate = jnp.dot(hbuf[...], ring[slot, :width, :], preferred_element_type=F32)
            slot = take(phase, layer, 2 * i + 1, 'u', i)
            up = jnp.dot(hbuf[...], ring[slot, :width, :], preferred_element_type=F32)
            ubuf[:, pl.ds(pl.multiple_of(i * TILE, TILE), TILE)] = (jax.nn.silu(gate) * up).astype(BF16)
            return carry

        lax.fori_loop(first, last, body, 0)

    for g in range(AHEAD):
        p = max(k for k in range(len(phases)) if bases[k] <= g)
        start_tile(p, 0, g - bases[p], g)
    x_load = pltpu.make_async_copy(x_hbm, xbuf, load_sem.at[0])
    kv_load = pltpu.make_async_copy(kv_hbm, kvbuf, load_sem.at[1])
    x_load.start()
    kv_load.start()

    barrier = pltpu.get_barrier_semaphore()
    pl.semaphore_signal(barrier, inc=1, device_id={'heads': other}, device_id_type=MESH)
    pl.semaphore_wait(barrier, 1)

    x_load.wait()
    kv_load.wait()

    a_cut = min(n_f, 20)
    b_cut = min(n_f, 10)

    def layer_body(layer, carry):
        @pl.when(layer > 0)
        def _():
            shared(0)
        norm(0, ga_ref, layer)
        project(0, 0, layer)

        @pl.when(layer > 0)
        def _():
            reduce_and_share(1)
        attend(0, layer)
        reduce_out(3, 0, layer, 'o', abuf, q_rows)

        @pl.when(layer > 0)
        def _():
            shared(1)
        norm(1, ga_ref, layer)
        project(4, 1, layer)
        attend(1, layer)
        reduce_and_share(0)
        reduce_out(7, 1, layer, 'o', abuf, q_rows)
        shared(0)
        norm(0, gm_ref, layer)
        gate_up(8, layer, 0, a_cut)
        reduce_and_share(1)
        gate_up(8, layer, a_cut, n_f)
        reduce_out(9, 0, layer, 'd', ubuf, ffn)
        shared(1)
        norm(1, gm_ref, layer)
        gate_up(10, layer, 0, b_cut)
        reduce_and_share(0)
        gate_up(10, layer, b_cut, n_f)
        reduce_out(11, 1, layer, 'd', ubuf, ffn)
        return carry

    lax.fori_loop(0, layers, layer_body, 0)
    shared(0)
    first = pltpu.make_async_copy(xbuf.at[pl.ds(0, rows), :], out_hbm.at[pl.ds(0, rows), :], load_sem.at[0])
    first.start()
    reduce_and_share(1)
    shared(1)
    second = pltpu.make_async_copy(xbuf.at[pl.ds(rows, rows), :], out_hbm.at[pl.ds(rows, rows), :], load_sem.at[1])
    second.start()
    first.wait()
    second.wait()


def solution(mesh):
    owners = mesh.shape['pool']

    def local_fn(kv_pool, page_idx, x_tokens, gain_attn, w_q, w_k, w_v, w_o, gain_mlp, w_gate, w_up, w_down):
        layers, pages, _, page_len, kv_loc, head_dim = kv_pool.shape
        tokens, width = x_tokens.shape[1:]
        ffn = w_gate.shape[2]
        req_pages = page_idx.shape[2]
        q_loc = w_q.shape[2] // head_dim
        group_q = q_loc // kv_loc
        prefix = owners * req_pages * page_len
        rows = tokens // 2

        wanted = page_idx.reshape(owners * req_pages)
        wanted = (wanted[None, :] + pages * jnp.arange(layers, dtype=wanted.dtype)[:, None]).reshape(-1)
        flat = kv_pool.reshape(layers * pages, 2, page_len, kv_loc, head_dim)
        picked = jnp.take(flat, wanted, axis=0, mode='clip').reshape(layers, owners, req_pages, 2, page_len, kv_loc, head_dim)
        picked = picked.transpose(1, 0, 3, 5, 2, 4, 6).reshape(owners, layers * 2 * kv_loc, req_pages * page_len, head_dim)
        received = lax.all_to_all(picked, 'pool', 0, 0, tiled=True)
        kv_pre = received.transpose(1, 0, 2, 3).reshape(layers, 2, kv_loc, prefix, head_dim)

        cos_tab, sin_tab = rope_tables(prefix, tokens, head_dim)
        gains = [g.astype(F32).reshape(layers, 1, width) for g in (gain_attn, gain_mlp)]
        hbm = pl.BlockSpec(memory_space=pl.ANY)
        vmem = pl.BlockSpec(memory_space=pltpu.VMEM)
        dims = (layers, tokens, kv_loc, group_q, head_dim, width, ffn, prefix)
        weights = (w_q, w_k, w_v, w_o, w_gate, w_up, w_down)
        n_bytes = 2 * sum(w.size * 2 for w in weights)
        out = pl.pallas_call(
            functools.partial(layers_kernel, dims),
            out_shape=jax.ShapeDtypeStruct((tokens, width), BF16),
            in_specs=[hbm, hbm, vmem, vmem, vmem, vmem] + [hbm] * 7,
            out_specs=hbm,
            scratch_shapes=[
                pltpu.VMEM((SLOTS, max(ffn, width), TILE), BF16),
                pltpu.VMEM((tokens, width), BF16),
                pltpu.VMEM((rows, width), BF16),
                pltpu.VMEM((q_loc, rows, head_dim), BF16),
                pltpu.VMEM((kv_loc, tokens, head_dim), BF16),
                pltpu.VMEM((kv_loc, tokens, head_dim), BF16),
                pltpu.VMEM((rows, q_loc * head_dim), BF16),
                pltpu.VMEM((rows, ffn), BF16),
                pltpu.VMEM((2, rows, width), F32),
                pltpu.VMEM((2, rows // 2, width), F32),
                pltpu.VMEM((layers, 2, kv_loc, prefix, head_dim), BF16),
                pltpu.SemaphoreType.DMA((SLOTS,)),
                pltpu.SemaphoreType.DMA((2,)),
                pltpu.SemaphoreType.DMA((2,)),
                pltpu.SemaphoreType.DMA((2,)),
                pltpu.SemaphoreType.DMA((2,)),
                pltpu.SemaphoreType.DMA((2,)),
            ],
            compiler_params=pltpu.CompilerParams(collective_id=0, has_side_effects=True, vmem_limit_bytes=62 * 1024 * 1024),
            cost_estimate=pl.CostEstimate(flops=tokens * n_bytes // 2, bytes_accessed=n_bytes, transcendentals=0),
        )(kv_pre, x_tokens[0], cos_tab, sin_tab, *gains, *weights)
        return out[None]

    pool_spec = P(None, ('rep', 'pool'), None, None, 'heads', None)
    index_spec = P('rep', 'pool', None)
    x_spec = P(('rep', 'pool'), None, None)
    gain_spec = P(None, None)
    col_spec = P(None, None, 'heads')
    row_spec = P(None, 'heads', None)
    return jax.shard_map(local_fn, mesh=mesh, in_specs=(pool_spec, index_spec, x_spec, gain_spec, col_spec, col_spec, col_spec, row_spec, gain_spec, col_spec, col_spec, row_spec), out_specs=x_spec, check_vma=False)
```

time: 966 us -> 482 us (0.50)
  waiting for transfers between devices: 451 us -> 22.8 us
  Pallas kernels: 0 us -> 421 us
  matrix products: 283 us -> 0 us
  local copies, waits for them, and re-layouts: 172 us -> 30.5 us
  other arithmetic: 32 us -> 2.14 us
  between operations: 14.1 us -> 0.04 us
    psum x4 -> x0, waiting for transfers between devices: 450 us -> none  [the longest x2 251 us: local_fn(): lax.psum(jnp.dot(attn_cat, w_o[layer_id], preferred_element_type=jnp.floa...]
    pallas_call x0 -> x1, Pallas kernels: none -> 421 us  [local_fn(): pl.pallas_call(functools.partial(layers_kernel, dims), out_shape=jax.Shap...]
    dot_general x22 -> x0, matrix products: 283 us -> none  [the longest x2 66 us: local_fn(): jnp.dot(h_mlp, w_gate[layer_id], preferred_element_type=jnp.float32)]
    dot_general x6 -> x0, local copies, waits for them, and re-layouts: 130 us -> none  [the longest x3 105 us: local_fn(): jnp.dot(h_att, w_q[layer_id], preferred_element_type=jnp.float32)]
    all_to_all x2 -> x1, waiting for transfers between devices: 0.01 us -> 22.8 us  [local_fn(): received = lax.all_to_all(picked, 'pool', 0, 0, tiled=True)]
    reduce_sum x8 -> x0, other arithmetic: 19.1 us -> none  [the longest x4 13.5 us: rms_norm(): jnp.mean(hid_f32 * hid_f32, axis=-1, keepdims=True) + 1e-05]
    slice x7 -> x0, local copies, waits for them, and re-layouts: 15.4 us -> none  [the longest x1 11.1 us: local_fn(): picked = jnp.take(kv_pool[layer_id], wanted, axis=0)]
    unnamed x45 -> x9, local copies, waits for them, and re-layouts: 4.23 us -> 19 us
  transfers between devices with their start and end apart: 6 -> 1, of which waited for: 4 -> 1; matrix products, arithmetic and copies ran while one was open for 17% -> 1% of each run, Pallas kernels for 0% -> 0%
where the time goes in v1:
time: 482 us
  Pallas kernels  421 us (87%)
  local copies, waits for them, and re-layouts  30.5 us (6%)
  waiting for transfers between devices  22.8 us (5%)
    pallas_call x1, Pallas kernels, local_fn(): pl.pallas_call(functools.partial(layers_kernel, dims), out_shape=jax.Shap...  421 us
    all_to_all x1, waiting for transfers between devices, local_fn(): received = lax.all_to_all(picked, 'pool', 0, 0, tiled=True)  22.8 us
    unnamed x9, local copies, waits for them, and re-layouts  19 us
  transfers between devices with their start and end apart: 1, of which 1 were waited for; matrix products, arithmetic and copies ran while one was open for 1% of the time, Pallas kernels for 0%

profile of v1, /device:TPU:0, one launch (start us, length us, event | category | flops | bytes accessed | tf_op | source)
XLA Modules:
  0.0 481.6 jit_solution(757894102077421932)
XLA Ops:
  0.0 0.0 copy-start.2
  0.0 15.1 %copy.16 = bf16[2,128,2,32,4,128]{5,3,4,2,1,0:T(8,128)(2,1)} copy(bf16[2,128,2,32,4,128]{5,4,3,2,1,0:T(4,128)(2,1)} %param.12) | data formatting | bytes 33554432 | tf_op args[0]
  15.1 0.0 copy-start
  15.1 0.0 copy-start.1
  15.1 0.5 broadcast.36
  15.6 0.0 copy-done.2
  15.6 0.7 reduce.3
  16.3 0.1 add.41
  16.4 0.1 broadcast_add_fusion
  16.4 0.1 reshape.77
  16.5 6.7 %gather_fusion = bf16[32,2,32,4,128]{4,2,3,1,0:T(8,128)(2,1)S(1)} fusion(bf16[256,2,32,4,128]{4,2,3,1,0:T(8,128)(2,1)} %bitcast.9, s32[1024]{0:T(1024)S(1)} %pad_clamp_fusion), kind=kCustom, calls=%fused_computation | custom fusion | bytes 4194432 | tf_op jit(solution)/shard_map/jit(_take)/gather | solution.py:330
  23.3 1.9 copy.17
  25.2 4.6 all-to-all-start
  29.8 0.0 copy-done
  29.8 0.6 reshape.72.ga_ref
  30.4 0.0 copy-done.1
  30.4 0.6 reshape.74.gm_ref
  31.1 0.5 fusion
  31.6 0.8 pad_maximum_fusion
  32.5 22.8 %all-to-all-done = bf16[4,16,128,128]{3,2,1,0:T(8,128)(2,1)S(1)} async-done(((bf16[4,16,128,128]{3,2,1,0:T(8,128)(2,1)}), bf16[4,16,128,128]{3,2,1,0:T(8,128)(2,1)S(1)}, u32[]{:S(2)}, u32[]{:S(2)}) %all-to-all-start) | async-done | bytes 2097184 | tf_op jit(solution)/shard_map/all_to_all | solution.py:332
  55.3 1.5 copy.18
  56.7 421.4 %shard_map.118 = bf16[256,5120]{1,0:T(8,128)(2,1)} custom-call(bf16[2,2,4,512,128]{4,3,2,1,0:T(8,128)(2,1)} %bitcast.11, bf16[256,5120]{1,0:T(8,128)(2,1)} %bitcast.15, f32[256,128]{1,0:T(8,128)} %get-tuple-element.8.cos_ref, f32[256,128]{1,0:T(8,128)} %get-tuple-element.9.sin_ref, f32[2,1,5120]{2,1,0:T(1,128)} %reshape.72.ga_ref, ...), custom_call_target="tpu_custom_call" | custom-call | flops 140928614400 | bytes 1101004800 | tf_op jit(solution)/shard_map/pallas_call | solution.py:342
  478.2 3.4 copy.20
  (4 shorter events, 0.0 us)
Async XLA Ops:
  0.0 15.6 %copy-start.2 = (s32[4,1,4]{2,1,0:T(1,128)S(1)}, s32[4,1,4]{2,1,0:T(1,128)}, u32[]{:S(2)}) copy-start(s32[4,1,4]{2,1,0:T(1,128)} %param.13) | copy-start | bytes 196
  15.1 14.7 %copy-start = (bf16[2,5120]{1,0:T(2,128)(2,1)S(1)}, bf16[2,5120]{1,0:T(2,128)(2,1)}, u32[]{:S(2)}) copy-start(bf16[2,5120]{1,0:T(2,128)(2,1)} %param.15) | copy-start | bytes 61444
  15.1 15.3 %copy-start.1 = (bf16[2,5120]{1,0:T(2,128)(2,1)S(1)}, bf16[2,5120]{1,0:T(2,128)(2,1)}, u32[]{:S(2)}) copy-start(bf16[2,5120]{1,0:T(2,128)(2,1)} %param.20) | copy-start | bytes 61444
  25.2 30.1 %all-to-all-start = ((bf16[4,16,128,128]{3,2,1,0:T(8,128)(2,1)}), bf16[4,16,128,128]{3,2,1,0:T(8,128)(2,1)S(1)}, u32[]{:S(2)}, u32[]{:S(2)}) async-start(bf16[4,16,128,128]{3,2,1,0:T(8,128)(2,1)} %bitcast.13), calls=%async_computation | async-start | bytes 4194304 | tf_op jit(solution)/shard_map/all_to_all | solution.py:332

commit v2 on v1

--- a/solution.py
+++ b/solution.py
@@ -29,9 +29,9 @@
     wq_hbm, wk_hbm, wv_hbm, wo_hbm, wg_hbm, wu_hbm, wd_hbm,
     out_hbm,
     ring, xbuf, hbuf, qbuf, kbuf, vbuf, abuf, ubuf, pbuf, rbuf, kvbuf,
-    ring_sem, load_sem, rs_send, rs_recv, ag_send, ag_recv,
+    ring_sem, load_sem, rs_send, rs_recv, ag_send, ag_recv, kv_send, kv_recv,
 ):
-    layers, tokens, kv_loc, group_q, head_dim, width, ffn, prefix = dims
+    layers, tokens, kv_loc, group_q, head_dim, width, ffn, prefix, owners = dims
     q_loc = kv_loc * group_q
     rows = tokens // 2
     half = rows // 2
@@ -40,6 +40,8 @@
 
     me = lax.axis_index('heads')
     other = 1 - me
+    pool = lax.axis_index('pool')
+    own_len = prefix // owners
 
     n_q, n_kv = q_loc * head_dim // TILE, kv_loc * head_dim // TILE
     n_d, n_f = width // TILE, ffn // TILE
@@ -162,7 +164,7 @@
         def body(g, carry):
             for r in range(group_q):
                 q = qbuf[g * group_q + r]
-                s_pre = lax.dot_general(q, kvbuf[layer, 0, g], nt, preferred_element_type=F32) * scale
+                s_pre = lax.dot_general(q, kvbuf[layer, g], nt, preferred_element_type=F32) * scale
                 s_new = lax.dot_general(q, kbuf[g, :n_new, :], nt, preferred_element_type=F32) * scale
                 tok = chunk * rows + lax.broadcasted_iota(jnp.int32, (rows, n_new), 0)
                 key = lax.broadcasted_iota(jnp.int32, (rows, n_new), 1)
@@ -171,7 +173,7 @@
                 e_pre = jnp.exp(s_pre - top)
                 e_new = jnp.exp(s_new - top)
                 inv = 1.0 / (jnp.sum(e_pre, axis=-1, keepdims=True) + jnp.sum(e_new, axis=-1, keepdims=True))
-                att = jnp.dot((e_pre * inv).astype(BF16), kvbuf[layer, 1, g], preferred_element_type=F32)
+                att = jnp.dot((e_pre * inv).astype(BF16), kvbuf[layer, kv_loc + g], preferred_element_type=F32)
                 att = att + jnp.dot((e_new * inv).astype(BF16), vbuf[g, :n_new, :], preferred_element_type=F32)
                 col = pl.multiple_of((g * group_q + r) * head_dim, head_dim)
                 abuf[:, pl.ds(col, head_dim)] = att.astype(BF16)
@@ -246,20 +248,44 @@
 
         lax.fori_loop(first, last, body, 0)
 
+    def page_place(layer):
+        return kvbuf.at[layer, :, pl.ds(pl.multiple_of(pool * own_len, own_len), own_len), :]
+
+    def page_send(layer, step):
+        to = lax.rem(pool + step, owners)
+        return pltpu.make_async_remote_copy(
+            src_ref=kv_hbm.at[layer, to],
+            dst_ref=page_place(layer),
+            send_sem=kv_send.at[layer, step],
+            recv_sem=kv_recv.at[layer, step],
+            device_id={'pool': to},
+            device_id_type=MESH,
+        )
+
+    def page_keep(layer):
+        return pltpu.make_async_copy(kv_hbm.at[layer, pool], page_place(layer), kv_send.at[layer, 0])
+
+    def pages_wait(layer):
+        page_keep(layer).wait()
+        for step in range(1, owners):
+            page_send(layer, step).wait()
+
     for g in range(AHEAD):
         p = max(k for k in range(len(phases)) if bases[k] <= g)
         start_tile(p, 0, g - bases[p], g)
     x_load = pltpu.make_async_copy(x_hbm, xbuf, load_sem.at[0])
-    kv_load = pltpu.make_async_copy(kv_hbm, kvbuf, load_sem.at[1])
     x_load.start()
-    kv_load.start()
 
     barrier = pltpu.get_barrier_semaphore()
     pl.semaphore_signal(barrier, inc=1, device_id={'heads': other}, device_id_type=MESH)
-    pl.semaphore_wait(barrier, 1)
-
+    for step in range(1, owners):
+        pl.semaphore_signal(barrier, inc=1, device_id={'pool': lax.rem(pool + step, owners)}, device_id_type=MESH)
+    pl.semaphore_wait(barrier, owners)
+    for layer in range(layers):
+        for step in range(1, owners):
+            page_send(layer, step).start()
+        page_keep(layer).start()
     x_load.wait()
-    kv_load.wait()
 
     a_cut = min(n_f, 20)
     b_cut = min(n_f, 10)
@@ -274,6 +300,7 @@
         @pl.when(layer > 0)
         def _():
             reduce_and_share(1)
+        pages_wait(layer)
         attend(0, layer)
         reduce_out(3, 0, layer, 'o', abuf, q_rows)
 
@@ -311,6 +338,20 @@
     second.wait()
 
 
+def pick_kernel(idx_ref, pool_hbm, out_ref, sems):
+    layers, wanted = out_ref.shape[:2]
+
+    def page(layer, i):
+        return pltpu.make_async_copy(pool_hbm.at[layer, idx_ref[i]], out_ref.at[layer, i], sems.at[layer, i])
+
+    for layer in range(layers):
+        for i in range(wanted):
+            page(layer, i).start()
+    for layer in range(layers):
+        for i in range(wanted):
+            page(layer, i).wait()
+
+
 def solution(mesh):
     owners = mesh.shape['pool']
 
@@ -325,18 +366,21 @@
         rows = tokens // 2
 
         wanted = page_idx.reshape(owners * req_pages)
-        wanted = (wanted[None, :] + pages * jnp.arange(layers, dtype=wanted.dtype)[:, None]).reshape(-1)
-        flat = kv_pool.reshape(layers * pages, 2, page_len, kv_loc, head_dim)
-        picked = jnp.take(flat, wanted, axis=0, mode='clip').reshape(layers, owners, req_pages, 2, page_len, kv_loc, head_dim)
-        picked = picked.transpose(1, 0, 3, 5, 2, 4, 6).reshape(owners, layers * 2 * kv_loc, req_pages * page_len, head_dim)
-        received = lax.all_to_all(picked, 'pool', 0, 0, tiled=True)
-        kv_pre = received.transpose(1, 0, 2, 3).reshape(layers, 2, kv_loc, prefix, head_dim)
+        picked = pl.pallas_call(
+            pick_kernel,
+            out_shape=jax.ShapeDtypeStruct((layers, owners * req_pages) + kv_pool.shape[2:], BF16),
+            in_specs=[pl.BlockSpec(memory_space=pltpu.SMEM), pl.BlockSpec(memory_space=pl.ANY)],
+            out_specs=pl.BlockSpec(memory_space=pltpu.VMEM),
+            scratch_shapes=[pltpu.SemaphoreType.DMA((layers, owners * req_pages))],
+        )(wanted, kv_pool)
+        picked = picked.reshape(layers, owners, req_pages, 2, page_len, kv_loc, head_dim)
+        kv_pre = picked.transpose(0, 1, 3, 5, 2, 4, 6).reshape(layers, owners, 2 * kv_loc, req_pages * page_len, head_dim)
 
         cos_tab, sin_tab = rope_tables(prefix, tokens, head_dim)
         gains = [g.astype(F32).reshape(layers, 1, width) for g in (gain_attn, gain_mlp)]
         hbm = pl.BlockSpec(memory_space=pl.ANY)
         vmem = pl.BlockSpec(memory_space=pltpu.VMEM)
-        dims = (layers, tokens, kv_loc, group_q, head_dim, width, ffn, prefix)
+        dims = (layers, tokens, kv_loc, group_q, head_dim, width, ffn, prefix, owners)
         weights = (w_q, w_k, w_v, w_o, w_gate, w_up, w_down)
         n_bytes = 2 * sum(w.size * 2 for w in weights)
         out = pl.pallas_call(
@@ -355,13 +399,15 @@
                 pltpu.VMEM((rows, ffn), BF16),
                 pltpu.VMEM((2, rows, width), F32),
                 pltpu.VMEM((2, rows // 2, width), F32),
-                pltpu.VMEM((layers, 2, kv_loc, prefix, head_dim), BF16),
+                pltpu.VMEM((layers, 2 * kv_loc, prefix, head_dim), BF16),
                 pltpu.SemaphoreType.DMA((SLOTS,)),
                 pltpu.SemaphoreType.DMA((2,)),
                 pltpu.SemaphoreType.DMA((2,)),
                 pltpu.SemaphoreType.DMA((2,)),
                 pltpu.SemaphoreType.DMA((2,)),
                 pltpu.SemaphoreType.DMA((2,)),
+                pltpu.SemaphoreType.DMA((layers, owners)),
+                pltpu.SemaphoreType.DMA((layers, owners)),
             ],
             compiler_params=pltpu.CompilerParams(collective_id=0, has_side_effects=True, vmem_limit_bytes=62 * 1024 * 1024),
             cost_estimate=pl.CostEstimate(flops=tokens * n_bytes // 2, bytes_accessed=n_bytes, transcendentals=0),

time: 482 us -> 441 us (0.915)
  waiting for transfers between devices: 22.8 us -> 0 us
  local copies, waits for them, and re-layouts: 30.5 us -> 10.8 us
  Pallas kernels: 421 us -> 427 us
    all_to_all x1 -> x0, waiting for transfers between devices: 22.8 us -> none  [local_fn(): received = lax.all_to_all(picked, 'pool', 0, 0, tiled=True)]
    unnamed x9 -> x2, local copies, waits for them, and re-layouts: 19 us -> 3.92 us
    gather x1 -> x0, local copies, waits for them, and re-layouts: 6.72 us -> none  [local_fn(): jnp.take(flat, wanted, axis=0, mode='clip')]
  transfers between devices with their start and end apart: 1 -> 0, of which waited for: 1 -> 0; matrix products, arithmetic and copies ran while one was open for 1% -> 0% of each run, Pallas kernels for 0% -> 0%
where the time goes in v2:
time: 441 us
  Pallas kernels  427 us (97%)
  local copies, waits for them, and re-layouts  10.8 us (2%)
    pallas_call x1, Pallas kernels, local_fn(): pl.pallas_call(functools.partial(layers_kernel, dims), out_shape=jax.Shap...  423 us

profile of v2, /device:TPU:0, one launch (start us, length us, event | category | flops | bytes accessed | tf_op | source)
XLA Modules:
  0.0 440.7 jit_solution(9063357624443301276)
XLA Ops:
  0.0 0.5 broadcast.18
  0.5 1.3 reduce.3
  1.9 0.7 reshape.30.idx_ref
  2.5 1.4 reshape.38.ga_ref
  3.9 1.4 reshape.40.gm_ref
  5.3 0.5 fusion
  5.8 0.8 pad_maximum_fusion
  6.7 3.8 shard_map.118
  10.5 3.5 copy.13
  14.0 423.4 %shard_map.119 = bf16[256,5120]{1,0:T(8,128)(2,1)} custom-call(bf16[2,4,8,128,128]{4,3,2,1,0:T(8,128)(2,1)} %bitcast.7, bf16[256,5120]{1,0:T(8,128)(2,1)} %bitcast.9, f32[256,128]{1,0:T(8,128)} %get-tuple-element.8.cos_ref, f32[256,128]{1,0:T(8,128)} %get-tuple-element.9.sin_ref, f32[2,1,5120]{2,1,0:T(1,128)} %reshape.38.ga_ref, ...), custom_call_target="tpu_custom_call" | custom-call | flops 140928614400 | bytes 1101004800 | tf_op jit(solution)/shard_map/pallas_call | solution.py:386
  437.3 3.4 copy.15
  (2 shorter events, 0.0 us)

commit v3 on v2

--- a/solution.py
+++ b/solution.py
@@ -2,6 +2,7 @@
 
 import jax
 import jax.numpy as jnp
+import numpy as np
 from jax import lax
 from jax.experimental import pallas as pl
 from jax.experimental.pallas import tpu as pltpu
@@ -12,23 +13,26 @@
 BF16 = jnp.bfloat16
 TILE = 256
 SLOTS = 9
+PIECE = 1
 AHEAD = SLOTS - 1
 
 
 def rope_tables(prefix, tokens, head_dim):
-    positions = (prefix + jnp.arange(tokens)).astype(F32)
-    inv_freq = 10000.0 ** (-2.0 * jnp.arange(head_dim // 2).astype(F32) / head_dim)
-    angles = positions[:, None] * inv_freq[None, :]
-    cos_tab, sin_tab = jnp.cos(angles), jnp.sin(angles)
-    return jnp.concatenate([cos_tab, cos_tab], axis=-1), jnp.concatenate([-sin_tab, sin_tab], axis=-1)
+    positions = (prefix + np.arange(tokens)).astype(np.float32)
+    inv_freq = np.float32(10000.0) ** (np.float32(-2.0) * np.arange(head_dim // 2).astype(np.float32) / np.float32(head_dim))
+    angles = (positions[:, None] * inv_freq[None, :]).astype(np.float32)
+    cos_tab, sin_tab = np.cos(angles), np.sin(angles)
+    cos_tab = np.concatenate([cos_tab, cos_tab], axis=-1).astype(np.float32)
+    sin_tab = np.concatenate([-sin_tab, sin_tab], axis=-1).astype(np.float32)
+    return jnp.asarray(cos_tab), jnp.asarray(sin_tab)
 
 
 def layers_kernel(
     dims,
-    kv_hbm, x_hbm, cos_ref, sin_ref, ga_ref, gm_ref,
+    kv_hbm, x_hbm, cos_ref, sin_ref, ga_in, gm_in,
     wq_hbm, wk_hbm, wv_hbm, wo_hbm, wg_hbm, wu_hbm, wd_hbm,
     out_hbm,
-    ring, xbuf, hbuf, qbuf, kbuf, vbuf, abuf, ubuf, pbuf, rbuf, kvbuf,
+    ga_ref, gm_ref, ring, xbuf, hbuf, qbuf, kbuf, vbuf, abuf, ubuf, pbuf, rbuf, kvbuf,
     ring_sem, load_sem, rs_send, rs_recv, ag_send, ag_recv, kv_send, kv_recv,
 ):
     layers, tokens, kv_loc, group_q, head_dim, width, ffn, prefix, owners = dims
@@ -51,6 +55,7 @@
     bases = [sum(n for _, n in phases[:p]) for p in range(len(phases))]
     per_layer = sum(n for _, n in phases)
     q_rows = q_loc * head_dim
+    cols = width // 2
 
     def copies(kind, layer, idx, slot):
         def tile(w_hbm, depth, col):
@@ -77,13 +82,10 @@
         elif isinstance(idx, int):
             copies('gu'[idx % 2], layer, idx // 2, slot).start()
         else:
-            @pl.when(lax.rem(idx, 2) == 0)
-            def _():
-                copies('g', layer, idx // 2, slot).start()
-
-            @pl.when(lax.rem(idx, 2) == 1)
-            def _():
-                copies('u', layer, idx // 2, slot).start()
+            for part in range(2):
+                @pl.when(lax.rem(idx, 2) == part)
+                def _(part=part):
+                    copies('gu'[part], layer, idx // 2, slot).start()
 
     def prefetch(phase, layer, idx):
         slot = lax.rem(layer * per_layer + bases[phase] + idx + AHEAD, SLOTS)
@@ -181,61 +183,77 @@
 
         lax.fori_loop(0, kv_loc, body, 0)
 
-    def send_block(chunk, col, cols):
+    def send_block(chunk, part, col, n_cols):
         at = pl.multiple_of(other * half, half)
         return pltpu.make_async_remote_copy(
-            src_ref=pbuf.at[chunk, pl.ds(at, half), pl.ds(col, cols)],
-            dst_ref=rbuf.at[chunk, :, pl.ds(col, cols)],
-            send_sem=rs_send.at[chunk],
-            recv_sem=rs_recv.at[chunk],
+            src_ref=pbuf.at[chunk, pl.ds(at, half), pl.ds(col, n_cols)],
+            dst_ref=rbuf.at[chunk, :, pl.ds(col, n_cols)],
+            send_sem=rs_send.at[chunk, part],
+            recv_sem=rs_recv.at[chunk, part],
             device_id={'heads': other},
             device_id_type=MESH,
         )
 
-    def reduce_out(phase, chunk, layer, kind, src, depth):
+    piece = PIECE * TILE
+
+    def reduce_out(phase, chunk, layer):
+        kind = phases[phase][0]
+        src, depth = (ubuf, ffn) if kind == 'd' else (abuf, q_rows)
+
         def body(i, carry):
             slot = take(phase, layer, i, kind, i)
             res = jnp.dot(src[...], ring[slot, :depth, :], preferred_element_type=F32)
             pbuf[chunk, :, pl.ds(pl.multiple_of(i * TILE, TILE), TILE)] = res
 
-            @pl.when(i > 0)
+            @pl.when((i > 0) & (lax.rem(i, PIECE) == 0))
             def _():
-                send_block(chunk, pl.multiple_of((i - 1) * TILE, TILE), TILE).start()
+                col = pl.multiple_of((i - PIECE) * TILE, TILE)
+
+                @pl.when(i * TILE <= cols)
+                def _():
+                    send_block(chunk, 0, col, piece).start()
+
+                @pl.when(i * TILE > cols)
+                def _():
+                    send_block(chunk, 1, col, piece).start()
             return carry
 
         lax.fori_loop(0, n_d, body, 0)
-        send_block(chunk, width - TILE, TILE).start()
-
-    def share(chunk):
+        send_block(chunk, 1, width - piece, piece).start()
+
+    def share(chunk, part):
         at = pl.multiple_of(chunk * rows + me * half, half)
+        place = xbuf.at[pl.ds(at, half), pl.ds(part * cols, cols)]
         return pltpu.make_async_remote_copy(
-            src_ref=xbuf.at[pl.ds(at, half), :],
-            dst_ref=xbuf.at[pl.ds(at, half), :],
-            send_sem=ag_send.at[chunk],
-            recv_sem=ag_recv.at[chunk],
+            src_ref=place,
+            dst_ref=place,
+            send_sem=ag_send.at[chunk, part],
+            recv_sem=ag_recv.at[chunk, part],
             device_id={'heads': other},
             device_id_type=MESH,
         )
 
-    def reduce_and_share(chunk):
-        whole = send_block(chunk, 0, width)
+    def reduce_and_share(chunk, part):
+        whole = send_block(chunk, part, part * cols, cols)
         whole.wait_recv()
         step = 16
+        side = slice(part * cols, (part + 1) * cols)
 
         def body(i, carry):
             at = pl.multiple_of(chunk * rows + me * half + i * step, step)
             mine = pl.multiple_of(me * half + i * step, step)
             got = pl.multiple_of(i * step, step)
-            total = pbuf[chunk, pl.ds(mine, step), :] + rbuf[chunk, pl.ds(got, step), :]
-            xbuf[pl.ds(at, step), :] = (xbuf[pl.ds(at, step), :].astype(F32) + total).astype(BF16)
+            total = pbuf[chunk, pl.ds(mine, step), side] + rbuf[chunk, pl.ds(got, step), side]
+            xbuf[pl.ds(at, step), side] = (xbuf[pl.ds(at, step), side].astype(F32) + total).astype(BF16)
             return carry
 
         lax.fori_loop(0, half // step, body, 0)
         whole.wait_send()
-        share(chunk).start()
+        share(chunk, part).start()
 
     def shared(chunk):
-        share(chunk).wait()
+        share(chunk, 0).wait()
+        share(chunk, 1).wait()
 
     def gate_up(phase, layer, first, last):
         def body(i, carry):
@@ -285,24 +303,36 @@
         for step in range(1, owners):
             page_send(layer, step).start()
         page_keep(layer).start()
+    for layer in range(layers):
+        ga_ref[layer] = ga_in[layer:layer + 1, :].astype(F32)
+        gm_ref[layer] = gm_in[layer:layer + 1, :].astype(F32)
     x_load.wait()
 
     a_cut = min(n_f, 20)
     b_cut = min(n_f, 10)
 
+    def served_gate_up(phase, layer, cut, chunk):
+        gate_up(phase, layer, 0, cut)
+        reduce_and_share(chunk, 0)
+        reduce_and_share(chunk, 1)
+        gate_up(phase, layer, cut, n_f)
+
     def layer_body(layer, carry):
+        def serve(part):
+            @pl.when(layer > 0)
+            def _():
+                reduce_and_share(1, part)
+
         @pl.when(layer > 0)
         def _():
             shared(0)
         norm(0, ga_ref, layer)
         project(0, 0, layer)
-
-        @pl.when(layer > 0)
-        def _():
-            reduce_and_share(1)
+        serve(0)
+        serve(1)
         pages_wait(layer)
         attend(0, layer)
-        reduce_out(3, 0, layer, 'o', abuf, q_rows)
+        reduce_out(3, 0, layer)
 
         @pl.when(layer > 0)
         def _():
@@ -310,27 +340,25 @@
         norm(1, ga_ref, layer)
         project(4, 1, layer)
         attend(1, layer)
-        reduce_and_share(0)
-        reduce_out(7, 1, layer, 'o', abuf, q_rows)
+        reduce_and_share(0, 0)
+        reduce_and_share(0, 1)
+        reduce_out(7, 1, layer)
         shared(0)
         norm(0, gm_ref, layer)
-        gate_up(8, layer, 0, a_cut)
-        reduce_and_share(1)
-        gate_up(8, layer, a_cut, n_f)
-        reduce_out(9, 0, layer, 'd', ubuf, ffn)
+        served_gate_up(8, layer, a_cut, 1)
+        reduce_out(9, 0, layer)
         shared(1)
         norm(1, gm_ref, layer)
-        gate_up(10, layer, 0, b_cut)
-        reduce_and_share(0)
-        gate_up(10, layer, b_cut, n_f)
-        reduce_out(11, 1, layer, 'd', ubuf, ffn)
+        served_gate_up(10, layer, b_cut, 0)
+        reduce_out(11, 1, layer)
         return carry
 
     lax.fori_loop(0, layers, layer_body, 0)
     shared(0)
     first = pltpu.make_async_copy(xbuf.at[pl.ds(0, rows), :], out_hbm.at[pl.ds(0, rows), :], load_sem.at[0])
     first.start()
-    reduce_and_share(1)
+    reduce_and_share(1, 0)
+    reduce_and_share(1, 1)
     shared(1)
     second = pltpu.make_async_copy(xbuf.at[pl.ds(rows, rows), :], out_hbm.at[pl.ds(rows, rows), :], load_sem.at[1])
     second.start()
@@ -340,9 +368,10 @@
 
 def pick_kernel(idx_ref, pool_hbm, out_ref, sems):
     layers, wanted = out_ref.shape[:2]
+    req_pages = idx_ref.shape[2]
 
     def page(layer, i):
-        return pltpu.make_async_copy(pool_hbm.at[layer, idx_ref[i]], out_ref.at[layer, i], sems.at[layer, i])
+        return pltpu.make_async_copy(pool_hbm.at[layer, idx_ref[i // req_pages, 0, i % req_pages]], out_ref.at[layer, i], sems.at[layer, i])
 
     for layer in range(layers):
         for i in range(wanted):
@@ -365,19 +394,17 @@
         prefix = owners * req_pages * page_len
         rows = tokens // 2
 
-        wanted = page_idx.reshape(owners * req_pages)
         picked = pl.pallas_call(
             pick_kernel,
             out_shape=jax.ShapeDtypeStruct((layers, owners * req_pages) + kv_pool.shape[2:], BF16),
             in_specs=[pl.BlockSpec(memory_space=pltpu.SMEM), pl.BlockSpec(memory_space=pl.ANY)],
             out_specs=pl.BlockSpec(memory_space=pltpu.VMEM),
             scratch_shapes=[pltpu.SemaphoreType.DMA((layers, owners * req_pages))],
-        )(wanted, kv_pool)
+        )(page_idx, kv_pool)
         picked = picked.reshape(layers, owners, req_pages, 2, page_len, kv_loc, head_dim)
         kv_pre = picked.transpose(0, 1, 3, 5, 2, 4, 6).reshape(layers, owners, 2 * kv_loc, req_pages * page_len, head_dim)
 
         cos_tab, sin_tab = rope_tables(prefix, tokens, head_dim)
-        gains = [g.astype(F32).reshape(layers, 1, width) for g in (gain_attn, gain_mlp)]
         hbm = pl.BlockSpec(memory_space=pl.ANY)
         vmem = pl.BlockSpec(memory_space=pltpu.VMEM)
         dims = (layers, tokens, kv_loc, group_q, head_dim, width, ffn, prefix, owners)
@@ -389,6 +416,8 @@
             in_specs=[hbm, hbm, vmem, vmem, vmem, vmem] + [hbm] * 7,
             out_specs=hbm,
             scratch_shapes=[
+                pltpu.VMEM((layers, 1, width), F32),
+                pltpu.VMEM((layers, 1, width), F32),
                 pltpu.VMEM((SLOTS, max(ffn, width), TILE), BF16),
                 pltpu.VMEM((tokens, width), BF16),
                 pltpu.VMEM((rows, width), BF16),
@@ -402,16 +431,16 @@
                 pltpu.VMEM((layers, 2 * kv_loc, prefix, head_dim), BF16),
                 pltpu.SemaphoreType.DMA((SLOTS,)),
                 pltpu.SemaphoreType.DMA((2,)),
-                pltpu.SemaphoreType.DMA((2,)),
-                pltpu.SemaphoreType.DMA((2,)),
-                pltpu.SemaphoreType.DMA((2,)),
-                pltpu.SemaphoreType.DMA((2,)),
+                pltpu.SemaphoreType.DMA((2, 2)),
+                pltpu.SemaphoreType.DMA((2, 2)),
+                pltpu.SemaphoreType.DMA((2, 2)),
+                pltpu.SemaphoreType.DMA((2, 2)),
                 pltpu.SemaphoreType.DMA((layers, owners)),
                 pltpu.SemaphoreType.DMA((layers, owners)),
             ],
             compiler_params=pltpu.CompilerParams(collective_id=0, has_side_effects=True, vmem_limit_bytes=62 * 1024 * 1024),
             cost_estimate=pl.CostEstimate(flops=tokens * n_bytes // 2, bytes_accessed=n_bytes, transcendentals=0),
-        )(kv_pre, x_tokens[0], cos_tab, sin_tab, *gains, *weights)
+        )(kv_pre, x_tokens[0], cos_tab, sin_tab, gain_attn, gain_mlp, *weights)
         return out[None]
 
     pool_spec = P(None, ('rep', 'pool'), None, None, 'heads', None)

time: 441 us -> 434 us (0.984)
  no operation moved by 1% of the time
where the time goes in v3:
time: 434 us; the launch traced here: 433 us
  Pallas kernels  426 us (98%)
  local copies, waits for them, and re-layouts  6.87 us (2%)
    pallas_call x1, Pallas kernels, local_fn(): pl.pallas_call(functools.partial(layers_kernel, dims), out_shape=jax.Shap...  423 us

profile of v3, /device:TPU:0, one launch (start us, length us, event | category | flops | bytes accessed | tf_op | source)
XLA Modules:
  0.0 433.3 jit_solution(7031105688875811072)
XLA Ops:
  0.0 3.8 shard_map.136
  3.9 3.5 copy.15
  7.3 422.6 %shard_map.137 = bf16[256,5120]{1,0:T(8,128)(2,1)} custom-call(bf16[2,4,8,128,128]{4,3,2,1,0:T(8,128)(2,1)} %bitcast.7, bf16[256,5120]{1,0:T(8,128)(2,1)} %bitcast.9, f32[256,128]{1,0:T(8,128)} %constant.4.clone.cos_ref, f32[256,128]{1,0:T(8,128)} %constant.5.clone.sin_ref, bf16[2,5120]{1,0:T(2,128)(2,1)} %ga_in.1, bf16[2,5120]{1,0:T(2,128)(2,1)} %gm_in.1, ...), custom_call_target="tpu_custom_call" | custom-call | flops 140928614400 | bytes 1101004800 | tf_op jit(solution)/shard_map/pallas_call | solution.py:413
  429.9 3.4 copy.17
